TPU v7x, 32 devices: a whole 2x2x4 slice. The times are simulated.
32 devices in a mesh: kpt: 2 (over y), row: 4 (over x, core), col: 4 (over z).
Axes of the slice: x: 2, y: 2, z: 4, core: 2. Of those that a mesh axis runs over, the one named last changes fastest.
Arguments:
- left_blocks: bfloat16 [8, 64, 2, 2, 128, 128], P(('kpt', 'row'), 'col'), parts along dimension 0, may hold values from -0.5 to 0.5
- left_rows: int32 [8, 64, 2], P(('kpt', 'row'), 'col'), parts along dimension 0, may hold values from 0 to 7, as said below
- left_count: int32 [8, 64], P(('kpt', 'row'), 'col'), parts along dimension 0, may hold values from 1 to 2, as said below
- left_level: int32 [8, 64, 2], P(('kpt', 'row'), 'col'), parts along dimension 0, may hold values from 0 to 7
- right_blocks: bfloat16 [2, 64, 4, 4, 2, 128, 128], P('kpt', 'row', 'col'), parts along dimension 0, may hold values from -6 to 6
- right_cols: int32 [2, 64, 4, 4], P('kpt', 'row', 'col'), parts along dimension 0, may hold values from 0 to 15, as said below
- right_count: int32 [2, 64, 4], P('kpt', 'row', 'col'), parts along dimension 0, may hold values from 1 to 4, as said below
- right_level: int32 [2, 64, 4, 4], P('kpt', 'row', 'col'), parts along dimension 0, may hold values from 0 to 7
Outputs:
- product_blocks: bfloat16 [64, 64, 2, 128, 128], P(('kpt', 'row'), 'col'), parts along dimension 0
There are 2 independent parts, one for each index of `kpt`. A program takes and returns all parts, laid end to end along the dimension named above; each array names one. Nothing has to cross between parts.
Inputs may be any that keep to these rules, and one draw needn't show every extreme that they name: `left_rows`: the 2 slots of one row group and block column name distinct block rows. `left_count`: in every row group some block column has all 2 slots live. `right_cols`: the 4 slots of one block row and column group name distinct block columns. `right_count`: in every column group some block row has all 4 slots live.
All inputs are finite; a program needn't handle non-finite values.
Results may differ from a plain program's by a relative error of at most 0.001.
Values may be sent and summed in bfloat16 or wider, within the bound.
A program may use at most 256 MiB of HBM per device.

v0:
```python
import jax
import jax.numpy as jnp
from jax import lax
from jax.sharding import PartitionSpec as P

GR = 8
LEVEL_CUT = 7


def pair_products(left_pack, right_pack, total):
    left_blocks, left_rows, left_count, left_level = left_pack
    right_blocks, right_cols, right_count, right_level = right_pack
    slots_left = left_rows.shape[1]
    slots_right = right_cols.shape[1]
    live_left = jnp.arange(slots_left, dtype=jnp.int32)[None, :] < left_count[:, None]
    live_right = jnp.arange(slots_right, dtype=jnp.int32)[None, :] < right_count[:, None]
    kept = live_left[:, :, None] & live_right[:, None, :]
    kept = kept & (left_level[:, :, None] + right_level[:, None, :] >= LEVEL_CUT)
    terms = jnp.einsum(
        "kmcij,kndjl->kmncdil", left_blocks, right_blocks, preferred_element_type=jnp.float32
    )
    real_part = terms[:, :, :, 0, 0] - terms[:, :, :, 1, 1]
    imag_part = terms[:, :, :, 0, 1] + terms[:, :, :, 1, 0]
    product = jnp.stack([real_part, imag_part], axis=3) * kept[:, :, :, None, None, None].astype(
        jnp.float32
    )
    row_index = jnp.broadcast_to(left_rows[:, :, None], kept.shape).reshape(-1)
    col_index = jnp.broadcast_to(right_cols[:, None, :], kept.shape).reshape(-1)
    width = left_blocks.shape[-1]
    return total.at[row_index, col_index].add(product.reshape(-1, 2, width, width))


def body(
    left_blocks,
    left_rows,
    left_count,
    left_level,
    right_blocks,
    right_cols,
    right_count,
    right_level,
):
    left_pack = (left_blocks[0], left_rows[0], left_count[0], left_level[0])
    right_pack = (
        right_blocks[:, :, 0],
        right_cols[:, :, 0],
        right_count[:, :, 0],
        right_level[:, :, 0],
    )
    width = left_blocks.shape[-1]
    panel_rows = left_blocks.shape[1]
    total = jnp.zeros((GR, panel_rows, 2, width, width), jnp.float32)
    whole = (
        lax.all_gather(right_pack[0], "row", axis=1, tiled=True),
        lax.all_gather(right_pack[1], "row", axis=1, tiled=True),
        lax.all_gather(right_pack[2], "row", axis=1, tiled=True),
        lax.all_gather(right_pack[3], "row", axis=1, tiled=True),
    )
    merged = whole[0].shape[0] * whole[0].shape[1]
    flat = jax.tree.map(lambda member: member.reshape((merged,) + member.shape[2:]), whole)
    carry = total
    piece = (
        lax.all_gather(left_pack[0], "col", axis=0, tiled=True),
        lax.all_gather(left_pack[1], "col", axis=0, tiled=True),
        lax.all_gather(left_pack[2], "col", axis=0, tiled=True),
        lax.all_gather(left_pack[3], "col", axis=0, tiled=True),
    )
    count = piece[0].shape[0]
    for first in range(0, count, panel_rows):
        size = min(panel_rows, count - first)
        left_part = jax.tree.map(lambda member: member[first : first + size], piece)
        right_part = jax.tree.map(
            lambda member: lax.dynamic_slice_in_dim(member, first, size, 0), flat
        )
        carry = pair_products(left_part, right_part, carry)
    total = carry
    return total.astype(jnp.bfloat16)


def solution(mesh):
    in_specs = (
        P(("kpt", "row"), "col", None, None, None, None),
        P(("kpt", "row"), "col", None),
        P(("kpt", "row"), "col"),
        P(("kpt", "row"), "col", None),
        P("kpt", "row", "col", None, None, None, None),
        P("kpt", "row", "col", None),
        P("kpt", "row", "col"),
        P("kpt", "row", "col", None),
    )
    out_specs = P(("kpt", "row"), "col", None, None, None)
    return jax.shard_map(body, mesh=mesh, in_specs=in_specs, out_specs=out_specs, check_vma=False)
```

profile of v0, /device:TPU:1, one launch (start us, length us, event | category | flops | bytes accessed | tf_op | source)
XLA Modules:
  0.0 728.5 jit_solution(17531730856529968428)
XLA Ops:
  6.5 0.7 all-gather.11.cloned.1.call-update
  7.3 0.7 all-gather.13.cloned.1.call-update
  8.0 1.2 dynamic-slice.1
  9.3 1.2 dynamic-slice
  11.7 0.8 copy.67
  12.4 0.8 copy.70
  13.2 11.6 %all-gather.6 = s32[1,64,2]{2,0,1:T(1,128)S(1)} all-gather(s32[1,16,2]{2,0,1:T(1,128)S(1)} %copy.67), channel_id=8, replica_groups=mesh['kpt'=2,'row'=4,'col'=4] {'col'}, dimensions={1}, use_global_device_ids=true | all-gather | bytes 640 | tf_op jit(solution)/shard_map/all_gather | solution.py:66
  24.8 0.7 bitcast_dynamic-update-slice_fusion
  25.5 7.5 %all-reduce.1 = s32[64]{0:T(128)S(1)} all-reduce(s32[64]{0:T(128)S(1)} %bitcast_dynamic-update-slice_fusion), channel_id=7, replica_groups=mesh['kpt'=2,'row'=4,'col'=4] {'row'}, use_global_device_ids=true, to_apply=%add.1 | all-reduce | flops 64 | bytes 512
  33.0 0.7 bitcast_dynamic-update-slice_fusion.1
  33.7 6.5 all-reduce
  40.2 7.5 %all-gather.7 = s32[1,64,1,4]{3,2,0,1:T(1,128)S(1)} all-gather(s32[1,16,1,4]{3,2,0,1:T(1,128)S(1)} %copy.70), channel_id=9, replica_groups=mesh['kpt'=2,'row'=4,'col'=4] {'row'}, dimensions={1}, use_global_device_ids=true | all-gather | bytes 1280 | tf_op jit(solution)/shard_map/all_gather | solution.py:57
  48.1 0.1 reshape.716
  48.3 0.8 copy.55
  49.0 10.2 %all-gather = s32[1,64,2]{2,0,1:T(1,128)S(1)} all-gather(s32[1,16,2]{2,0,1:T(1,128)S(1)} %copy.55), channel_id=2, replica_groups=mesh['kpt'=2,'row'=4,'col'=4] {'col'}, dimensions={1}, use_global_device_ids=true | all-gather | bytes 640 | tf_op jit(solution)/shard_map/all_gather | solution.py:64
  59.3 0.1 reshape.708
  59.5 0.8 copy.58
  60.2 8.3 %all-gather.1 = s32[1,64,1,4]{3,2,0,1:T(1,128)S(1)} all-gather(s32[1,16,1,4]{3,2,0,1:T(1,128)S(1)} %copy.58), channel_id=3, replica_groups=mesh['kpt'=2,'row'=4,'col'=4] {'row'}, dimensions={1}, use_global_device_ids=true | all-gather | bytes 1280 | tf_op jit(solution)/shard_map/all_gather | solution.py:55
  68.6 0.1 reshape.709
  68.8 0.1 reshape.717
  69.0 0.1 reshape.710
  69.1 0.1 reshape.711
  69.5 0.7 reshape.718
  70.3 0.1 reshape.712
  70.4 0.1 reshape.713
  70.7 0.7 reshape.719
  71.4 0.1 reshape.714
  71.7 0.6 fusion.4
  72.2 0.5 fusion.5
  72.8 0.5 fusion.6
  73.3 0.6 fusion.7
  73.9 43.8 %all-gather.11.cloned.1.call-done = bf16[1,64,1,4,2,128,128]{6,5,4,3,2,0,1:T(8,128)(2,1)} async-done(((bf16[1,16,1,4,2,128,128]{6,5,4,3,2,0,1:T(8,128)(2,1)}), bf16[1,64,1,4,2,128,128]{6,5,4,3,2,0,1:T(8,128)(2,1)}) %all-gather.11.cloned.1.call-update) | async-done | bytes 16777232 | tf_op jit(solution)/shard_map/all_gather | solution.py:54
  117.7 22.7 %copy.62 = bf16[1,64,1,4,2,128,128]{5,6,4,3,1,2,0:T(8,128)(2,1)} copy(bf16[1,64,1,4,2,128,128]{6,5,4,3,2,0,1:T(8,128)(2,1)} %all-gather.11.cloned.1.call-done) | data formatting | bytes 33554432 | tf_op jit(solution)/shard_map/all_gather | solution.py:54
  140.5 128.2 %all-gather.13.cloned.1.call-done = bf16[1,64,2,2,128,128]{5,4,3,2,0,1:T(8,128)(2,1)} async-done(((bf16[1,16,2,2,128,128]{5,4,3,2,0,1:T(8,128)(2,1)}), bf16[1,64,2,2,128,128]{5,4,3,2,0,1:T(8,128)(2,1)}) %all-gather.13.cloned.1.call-update) | async-done | bytes 8388624 | tf_op jit(solution)/shard_map/all_gather | solution.py:63
  268.7 18.5 %convolution_bitcast_fusion.3 = f32[16,2,4,2,2,128,128]{5,6,3,1,4,2,0:T(8,128)} fusion(bf16[1,64,4,2,128,128]{4,5,3,2,1,0:T(8,128)(2,1)} %bitcast.137, bf16[1,64,2,2,128,128]{5,4,3,2,1,0:T(8,128)(2,1)} %bitcast.149), kind=kOutput, calls=%fused_computation.11 | convolution fusion | flops 2147483648 | bytes 39845888 | tf_op jit(solution)/shard_map/kmcij,kndjl->kmncdil/dot_general | solution.py:19
  287.2 18.5 %convolution_bitcast_fusion.2 = f32[16,2,4,2,2,128,128]{5,6,3,1,4,2,0:T(8,128)} fusion(bf16[1,64,4,2,128,128]{4,5,3,2,1,0:T(8,128)(2,1)} %bitcast.138, bf16[1,64,2,2,128,128]{5,4,3,2,1,0:T(8,128)(2,1)} %bitcast.150), kind=kOutput, calls=%fused_computation.10 | convolution fusion | flops 2147483648 | bytes 39845888 | tf_op jit(solution)/shard_map/kmcij,kndjl->kmncdil/dot_general | solution.py:19
  305.6 18.7 %convolution_bitcast_fusion.1 = f32[16,2,4,2,2,128,128]{5,6,3,1,4,2,0:T(8,128)} fusion(bf16[1,64,4,2,128,128]{4,5,3,2,1,0:T(8,128)(2,1)} %bitcast.139, bf16[1,64,2,2,128,128]{5,4,3,2,1,0:T(8,128)(2,1)} %bitcast.151), kind=kOutput, calls=%fused_computation.9 | convolution fusion | flops 2147483648 | bytes 39845888 | tf_op jit(solution)/shard_map/kmcij,kndjl->kmncdil/dot_general | solution.py:19
  324.3 18.5 %convolution_bitcast_fusion = f32[16,2,4,2,2,128,128]{5,6,3,1,4,2,0:T(8,128)} fusion(bf16[1,64,4,2,128,128]{4,5,3,2,1,0:T(8,128)(2,1)} %bitcast.140, bf16[1,64,2,2,128,128]{5,4,3,2,1,0:T(8,128)(2,1)} %bitcast.152), kind=kOutput, calls=%fused_computation.8 | convolution fusion | flops 2147483648 | bytes 39845888 | tf_op jit(solution)/shard_map/kmcij,kndjl->kmncdil/dot_general | solution.py:19
  342.7 19.3 %slice_subtract_fusion.3 = (f32[16,2,4,1,1,128,128]{5,6,3,1,4,2,0:T(8,128)}, f32[16,2,4,1,1,128,128]{5,6,3,1,4,2,0:T(8,128)}) fusion(f32[16,2,4,2,2,128,128]{5,6,3,1,4,2,0:T(8,128)} %convolution_bitcast_fusion.3), kind=kLoop, calls=%fused_computation.19 | loop fusion | flops 4194304 | bytes 50331648 | tf_op jit(solution)/shard_map/sub | solution.py:22
  362.1 9.3 %copy.65 = f32[16,2,4,1,1,128,128]{6,5,2,1,0,4,3:T(8,128)} copy(f32[16,2,4,1,1,128,128]{5,6,3,1,4,2,0:T(8,128)} %get-tuple-element.11) | data formatting | bytes 16777216 | tf_op jit(solution)/shard_map/sub | solution.py:22
  371.4 9.2 %copy.66 = f32[16,2,4,1,1,128,128]{6,5,2,1,0,4,3:T(8,128)} copy(f32[16,2,4,1,1,128,128]{5,6,3,1,4,2,0:T(8,128)} %get-tuple-element.12) | data formatting | bytes 16777216 | tf_op jit(solution)/shard_map/add | solution.py:23
  380.6 6.8 maximum_multiply_fusion
  387.4 6.0 copy.73
  393.4 19.4 %slice_subtract_fusion.2 = (f32[16,2,4,1,1,128,128]{5,6,3,1,4,2,0:T(8,128)}, f32[16,2,4,1,1,128,128]{5,6,3,1,4,2,0:T(8,128)}) fusion(f32[16,2,4,2,2,128,128]{5,6,3,1,4,2,0:T(8,128)} %convolution_bitcast_fusion.2), kind=kLoop, calls=%fused_computation.17 | loop fusion | flops 4194304 | bytes 50331648 | tf_op jit(solution)/shard_map/sub | solution.py:22
  412.8 9.5 %copy.79 = f32[16,2,4,1,1,128,128]{6,5,2,1,0,4,3:T(8,128)} copy(f32[16,2,4,1,1,128,128]{5,6,3,1,4,2,0:T(8,128)} %get-tuple-element.9) | data formatting | bytes 16777216 | tf_op jit(solution)/shard_map/sub | solution.py:22
  422.3 9.2 %copy.80 = f32[16,2,4,1,1,128,128]{6,5,2,1,0,4,3:T(8,128)} copy(f32[16,2,4,1,1,128,128]{5,6,3,1,4,2,0:T(8,128)} %get-tuple-element.10) | data formatting | bytes 16777216 | tf_op jit(solution)/shard_map/add | solution.py:23
  431.5 6.8 maximum_multiply_fusion.1
  438.3 6.1 copy.85
  444.4 19.3 %slice_subtract_fusion.1 = (f32[16,2,4,1,1,128,128]{5,6,3,1,4,2,0:T(8,128)}, f32[16,2,4,1,1,128,128]{5,6,3,1,4,2,0:T(8,128)}) fusion(f32[16,2,4,2,2,128,128]{5,6,3,1,4,2,0:T(8,128)} %convolution_bitcast_fusion.1), kind=kLoop, calls=%fused_computation.15 | loop fusion | flops 4194304 | bytes 50331648 | tf_op jit(solution)/shard_map/sub | solution.py:22
  463.7 9.2 %copy.91 = f32[16,2,4,1,1,128,128]{6,5,2,1,0,4,3:T(8,128)} copy(f32[16,2,4,1,1,128,128]{5,6,3,1,4,2,0:T(8,128)} %get-tuple-element.7) | data formatting | bytes 16777216 | tf_op jit(solution)/shard_map/sub | solution.py:22
  473.0 9.2 %copy.92 = f32[16,2,4,1,1,128,128]{6,5,2,1,0,4,3:T(8,128)} copy(f32[16,2,4,1,1,128,128]{5,6,3,1,4,2,0:T(8,128)} %get-tuple-element.8) | data formatting | bytes 16777216 | tf_op jit(solution)/shard_map/add | solution.py:23
  482.2 6.8 maximum_multiply_fusion.2
  489.0 6.1 copy.97
  495.1 19.3 %slice_subtract_fusion = (f32[16,2,4,1,1,128,128]{5,6,3,1,4,2,0:T(8,128)}, f32[16,2,4,1,1,128,128]{5,6,3,1,4,2,0:T(8,128)}) fusion(f32[16,2,4,2,2,128,128]{5,6,3,1,4,2,0:T(8,128)} %convolution_bitcast_fusion), kind=kLoop, calls=%fused_computation.13 | loop fusion | flops 4194304 | bytes 50331648 | tf_op jit(solution)/shard_map/sub | solution.py:22
  514.4 9.2 %copy.103 = f32[16,2,4,1,1,128,128]{6,5,2,1,0,4,3:T(8,128)} copy(f32[16,2,4,1,1,128,128]{5,6,3,1,4,2,0:T(8,128)} %get-tuple-element.5) | data formatting | bytes 16777216 | tf_op jit(solution)/shard_map/sub | solution.py:22
  523.6 9.2 %copy.104 = f32[16,2,4,1,1,128,128]{6,5,2,1,0,4,3:T(8,128)} copy(f32[16,2,4,1,1,128,128]{5,6,3,1,4,2,0:T(8,128)} %get-tuple-element.6) | data formatting | bytes 16777216 | tf_op jit(solution)/shard_map/add | solution.py:23
  532.9 6.8 maximum_multiply_fusion.3
  539.7 6.0 copy.109
  545.7 7.9 %broadcast_in_dim.26 = f32[8,16,2,128,128]{4,3,2,1,0:T(8,128)} broadcast(f32[]{:T(128)} %constant.0.clone.1), dimensions={} | broadcast | bytes 16777220 | tf_op jit(solution)/shard_map/broadcast_in_dim | solution.py:52
  553.6 39.5 %scatter_fusion = f32[8,16,2,128,128]{4,3,2,1,0:T(8,128)} fusion(f32[8,16,2,128,128]{4,3,2,1,0:T(8,128)} %broadcast_in_dim.26, s32[128]{0:T(128)S(1)} %copy-done.3, f32[128,2,128,128]{3,2,1,0:T(8,128)} %copy.73), kind=kCustom, calls=%fused_computation | custom fusion | flops 4194304 | bytes 50332672 | tf_op jit(solution)/shard_map/scatter-add | solution.py:30
  593.0 39.8 %scatter_fusion.1 = f32[8,16,2,128,128]{4,3,2,1,0:T(8,128)} fusion(f32[8,16,2,128,128]{4,3,2,1,0:T(8,128)} %scatter_fusion, s32[128]{0:T(128)S(1)} %copy-done.2, f32[128,2,128,128]{3,2,1,0:T(8,128)} %copy.85), kind=kCustom, calls=%fused_computation.1 | custom fusion | flops 4194304 | bytes 50332672 | tf_op jit(solution)/shard_map/scatter-add | solution.py:30
  632.9 39.7 %scatter_fusion.2 = f32[8,16,2,128,128]{4,3,2,1,0:T(8,128)} fusion(f32[8,16,2,128,128]{4,3,2,1,0:T(8,128)} %scatter_fusion.1, s32[128]{0:T(128)S(1)} %copy-done.1, f32[128,2,128,128]{3,2,1,0:T(8,128)} %copy.97), kind=kCustom, calls=%fused_computation.2 | custom fusion | flops 4194304 | bytes 50332672 | tf_op jit(solution)/shard_map/scatter-add | solution.py:30
  672.5 39.7 %scatter_fusion.3 = f32[8,16,2,128,128]{4,3,2,1,0:T(8,128)} fusion(f32[8,16,2,128,128]{4,3,2,1,0:T(8,128)} %scatter_fusion.2, s32[128]{0:T(128)S(1)} %copy-done, f32[128,2,128,128]{3,2,1,0:T(8,128)} %copy.109), kind=kCustom, calls=%fused_computation.3 | custom fusion | flops 4194304 | bytes 50332672 | tf_op jit(solution)/shard_map/scatter-add | solution.py:30
  712.3 9.2 %convert_element_type.55 = bf16[8,16,2,128,128]{4,3,2,1,0:T(8,128)(2,1)} convert(f32[8,16,2,128,128]{4,3,2,1,0:T(8,128)} %scatter_fusion.3) | non-fusion elementwise | flops 4194304 | bytes 25165824 | tf_op jit(solution)/shard_map/convert_element_type | solution.py:77
  (39 shorter events, 1.4 us)
Async XLA Ops:
  6.5 111.2 %all-gather.11.cloned.1.call-start = ((), (), s32[]{:S(2)}) async-start(), calls=%async_computation | async-start | bytes 20971520 | tf_op jit(solution)/shard_map/all_gather | solution.py:54
  7.3 261.4 %all-gather.13.cloned.1.call-start = ((), (), s32[]{:S(2)}) async-start(), calls=%async_computation.1 | async-start | bytes 10485760 | tf_op jit(solution)/shard_map/all_gather | solution.py:63
  473.0 9.2 %copy-start.4 = (f32[128]{0:T(128)S(1)}, f32[128]{0:T(128)}, u32[]{:S(2)}) copy-start(f32[128]{0:T(128)} %reshape.718) | copy-start | bytes 1540
  523.6 9.2 %copy-start.5 = (f32[128]{0:T(128)S(1)}, f32[128]{0:T(128)}, u32[]{:S(2)}) copy-start(f32[128]{0:T(128)} %reshape.719) | copy-start | bytes 1540
  545.7 7.9 %copy-start.3 = (s32[128]{0:T(128)S(1)}, s32[128]{0:T(128)}, u32[]{:S(2)}) copy-start(s32[128]{0:T(128)} %fusion.4) | copy-start | bytes 1540
  553.6 39.5 %copy-start.2 = (s32[128]{0:T(128)S(1)}, s32[128]{0:T(128)}, u32[]{:S(2)}) copy-start(s32[128]{0:T(128)} %fusion.5) | copy-start | bytes 1540
  593.0 39.8 %copy-start.1 = (s32[128]{0:T(128)S(1)}, s32[128]{0:T(128)}, u32[]{:S(2)}) copy-start(s32[128]{0:T(128)} %fusion.6) | copy-start | bytes 1540
  632.9 39.7 %copy-start = (s32[128]{0:T(128)S(1)}, s32[128]{0:T(128)}, u32[]{:S(2)}) copy-start(s32[128]{0:T(128)} %fusion.7) | copy-start | bytes 1540
Sparse Core Ops, SparseCore 0:
  8.9 108.8 all-gather.10
  119.3 149.3 all-gather.12
where the time goes:
time: 733 us; the launch traced here: 729 us
  other arithmetic  275 us (38%)
  waiting for transfers between devices  173 us (24%)
  local copies, waits for them, and re-layouts  139 us (19%)
  matrix products  74 us (10%)
  blocking collectives  51.6 us (7%)
  between operations  15 us (2%)
    scatter-add x4, other arithmetic, pair_products(): total.at[row_index, col_index].add(product.reshape(-1, 2, width, width))  159 us
    all_gather x1, waiting for transfers between devices, body(): lax.all_gather(left_pack[0], 'col', axis=0, tiled=True)  128 us
    sub x4, other arithmetic, pair_products(): real_part = terms[:, :, :, 0, 0] - terms[:, :, :, 1, 1]  77.3 us
    dot_general x4, matrix products, pair_products(): jnp.einsum('kmcij,kndjl->kmncdil', left_blocks, right_blocks, preferred_e...  74 us
    all_gather x1, waiting for transfers between devices, body(): lax.all_gather(right_pack[0], 'row', axis=1, tiled=True)  43.8 us
    sub x4, local copies, waits for them, and re-layouts, pair_products(): real_part = terms[:, :, :, 0, 0] - terms[:, :, :, 1, 1]  37.2 us
    add x4, local copies, waits for them, and re-layouts, pair_products(): imag_part = terms[:, :, :, 0, 1] + terms[:, :, :, 1, 0]  37 us
    mul x4, other arithmetic, pair_products(): jnp.stack([real_part, imag_part], axis=3)  27.1 us
  transfers between devices with their start and end apart: 2, of which 2 were waited for; matrix products, arithmetic and copies ran while one was open for 5% of the time, Pallas kernels for 0%

commit v1 on v0

--- a/solution.py
+++ b/solution.py
@@ -1,3 +1,4 @@
+import functools
 import jax
 import jax.numpy as jnp
 from jax import lax
@@ -5,6 +6,36 @@
 
 GR = 8
 LEVEL_CUT = 7
+
+
+def _rest_sums_all(x_local, bus_axis):
+    arr_out = jax.lax.axis_size(bus_axis)
+    finding = jax.lax.axis_index(bus_axis)
+    wide_out, last, even = (arr_out, finding, x_local.shape[0])
+    to_i = 1
+    plain = lax.dynamic_update_slice_in_dim(
+        jnp.zeros(
+            tuple((h * wide_out if idx == 0 else h for idx, h in enumerate(x_local.shape))),
+            x_local.dtype,
+        ),
+        x_local,
+        last * even,
+        axis=0,
+    )
+    while to_i < wide_out:
+        x_local = jax.lax.ppermute(
+            x_local,
+            axis_name=bus_axis,
+            perm=tuple(((idx, (idx + 1) % wide_out) for idx in range(wide_out))),
+        )
+        plain = lax.dynamic_update_slice_in_dim(
+            plain, x_local, (last - to_i) % wide_out * even, axis=0
+        )
+        to_i = to_i + 1
+    return plain
+
+
+fit_entries = functools.partial(_rest_sums_all, bus_axis="col")
 
 
 def pair_products(left_pack, right_pack, total):
@@ -60,7 +91,7 @@
     flat = jax.tree.map(lambda member: member.reshape((merged,) + member.shape[2:]), whole)
     carry = total
     piece = (
-        lax.all_gather(left_pack[0], "col", axis=0, tiled=True),
+        fit_entries(left_pack[0]),
         lax.all_gather(left_pack[1], "col", axis=0, tiled=True),
         lax.all_gather(left_pack[2], "col", axis=0, tiled=True),
         lax.all_gather(left_pack[3], "col", axis=0, tiled=True),

time: 733 us -> 593 us (0.81)
  local copies, waits for them, and re-layouts: 139 us -> 37 us
  waiting for transfers between devices: 173 us -> 75 us
  blocking collectives: 51.6 us -> 88.1 us
  other arithmetic: 275 us -> 291 us
    all_gather x1 -> x0, waiting for transfers between devices: 128 us -> none  [body(): lax.all_gather(left_pack[0], 'col', axis=0, tiled=True)]
    ppermute x0 -> x3, waiting for transfers between devices: none -> 74.3 us  [_rest_sums_all(): jax.lax.ppermute(x_local, axis_name=bus_axis, perm=tuple(((idx, (idx + 1)...]
    all_gather x1, waiting for transfers between devices: 43.8 us -> 0.01 us  [body(): lax.all_gather(right_pack[0], 'row', axis=1, tiled=True)]
    all_gather x1, blocking collectives: 11.6 us -> 49.7 us  [body(): lax.all_gather(left_pack[3], 'col', axis=0, tiled=True)]
    sub x4 -> x0, local copies, waits for them, and re-layouts: 37.2 us -> none  [pair_products(): real_part = terms[:, :, :, 0, 0] - terms[:, :, :, 1, 1]]
    add x4 -> x0, local copies, waits for them, and re-layouts: 37 us -> none  [pair_products(): imag_part = terms[:, :, :, 0, 1] + terms[:, :, :, 1, 0]]
    mul x4 -> x0, local copies, waits for them, and re-layouts: 24.3 us -> none  [pair_products(): jnp.stack([real_part, imag_part], axis=3)]
    all_gather x1 -> x0, local copies, waits for them, and re-layouts: 22.7 us -> none  [body(): lax.all_gather(right_pack[0], 'row', axis=1, tiled=True)]
  transfers between devices with their start and end apart: 2 -> 4, of which waited for: 2 -> 2; matrix products, arithmetic and copies ran while one was open for 5% -> 5% of each run, Pallas kernels for 0% -> 0%
where the time goes in v1:
time: 593 us; the launch traced here: 582 us
  other arithmetic  291 us (49%)
  blocking collectives  88.1 us (15%)
  waiting for transfers between devices  75 us (13%)
  matrix products  74.1 us (12%)
  local copies, waits for them, and re-layouts  37 us (6%)
  between operations  15.2 us (3%)
    scatter-add x4, other arithmetic, pair_products(): total.at[row_index, col_index].add(product.reshape(-1, 2, width, width))  158 us
    sub x4, other arithmetic, pair_products(): real_part = terms[:, :, :, 0, 0] - terms[:, :, :, 1, 1]  77 us
    ppermute x3, waiting for transfers between devices, _rest_sums_all(): jax.lax.ppermute(x_local, axis_name=bus_axis, perm=tuple(((idx, (idx + 1)...  74.3 us
    dot_general x4, matrix products, pair_products(): jnp.einsum('kmcij,kndjl->kmncdil', left_blocks, right_blocks, preferred_e...  74.1 us
    all_gather x1, blocking collectives, body(): lax.all_gather(left_pack[3], 'col', axis=0, tiled=True)  49.7 us
    mul x4, other arithmetic, pair_products(): jnp.stack([real_part, imag_part], axis=3)  44 us
    unnamed x2, blocking collectives  14.4 us
  transfers between devices with their start and end apart: 4, of which 2 were waited for; matrix products, arithmetic and copies ran while one was open for 5% of the time, Pallas kernels for 0%

profile of v1, /device:TPU:1, one launch (start us, length us, event | category | flops | bytes accessed | tf_op | source)
XLA Modules:
  0.0 582.2 jit_solution(12254186339281514638)
XLA Ops:
  6.5 0.7 all-gather.9.cloned.1.call-update
  7.3 2.2 collective-permute-start
  9.4 1.2 dynamic-slice.1
  10.7 1.3 dynamic-slice
  13.3 0.8 bitcast_dynamic-update-slice_fusion
  14.1 43.0 %collective-permute-done = bf16[16,2,2,128,128]{4,3,2,1,0:T(8,128)(2,1)} collective-permute-done((bf16[16,2,2,128,128]{4,3,2,1,0:T(8,128)(2,1)}, bf16[16,2,2,128,128]{4,3,2,1,0:T(8,128)(2,1)}, u32[]{:S(2)}, u32[]{:S(2)}) %collective-permute-start) | collective-permute-done | bytes 2097184 | tf_op jit(solution)/shard_map/ppermute | solution.py:26
  57.1 0.7 bitcast_dynamic-update-slice_fusion.1
  57.8 0.8 copy.68
  58.6 0.8 copy.71
  59.4 0.8 copy.59
  60.1 0.8 copy.62
  60.9 49.7 %all-gather.5 = s32[1,64,2]{2,0,1:T(1,128)S(1)} all-gather(s32[1,16,2]{2,0,1:T(1,128)S(1)} %copy.68), channel_id=7, replica_groups=mesh['kpt'=2,'row'=4,'col'=4] {'col'}, dimensions={1}, use_global_device_ids=true | all-gather | bytes 640 | tf_op jit(solution)/shard_map/all_gather | solution.py:97
  110.5 10.5 %all-gather = s32[1,64,2]{2,0,1:T(1,128)S(1)} all-gather(s32[1,16,2]{2,0,1:T(1,128)S(1)} %copy.59), channel_id=2, replica_groups=mesh['kpt'=2,'row'=4,'col'=4] {'col'}, dimensions={1}, use_global_device_ids=true | all-gather | bytes 640 | tf_op jit(solution)/shard_map/all_gather | solution.py:95
  121.0 10.0 %all-reduce.1 = s32[64]{0:T(128)S(1)} all-reduce(s32[64]{0:T(128)S(1)} %bitcast_dynamic-update-slice_fusion), channel_id=6, replica_groups=mesh['kpt'=2,'row'=4,'col'=4] {'row'}, use_global_device_ids=true, to_apply=%add.1 | all-reduce | flops 64 | bytes 512
  131.0 4.4 all-reduce
  135.4 8.4 %all-gather.6 = s32[1,64,1,4]{3,2,0,1:T(1,128)S(1)} all-gather(s32[1,16,1,4]{3,2,0,1:T(1,128)S(1)} %copy.71), channel_id=8, replica_groups=mesh['kpt'=2,'row'=4,'col'=4] {'row'}, dimensions={1}, use_global_device_ids=true | all-gather | bytes 1280 | tf_op jit(solution)/shard_map/all_gather | solution.py:88
  143.8 5.2 all-gather.1
  149.3 0.1 and_convert_fusion.2
  149.5 0.1 and_convert_fusion.3
  149.7 0.1 reshape.717
  149.8 0.1 reshape.716
  149.9 0.1 broadcast_in_dim.29
  150.0 0.1 reshape.708
  150.1 0.1 reshape.709
  150.2 0.1 broadcast_in_dim.33
  150.3 0.1 reshape.710
  150.5 0.1 reshape.711
  150.6 0.1 iota_compare_fusion
  150.7 0.1 and_convert_fusion.1
  150.8 0.6 reshape.718
  151.5 0.1 reshape.712
  151.7 0.1 reshape.713
  151.8 0.1 broadcast_in_dim.39
  151.9 0.1 reshape.714
  152.0 0.1 reshape.715
  152.1 0.1 and_convert_fusion
  152.2 0.7 reshape.719
  152.9 0.5 fusion.4
  153.4 0.6 fusion.6
  154.0 5.5 broadcast_in_dim.32
  159.6 1.5 constant_dynamic-update-slice_fusion.3
  161.0 3.2 constant_dynamic-update-slice_fusion.2
  164.2 3.2 constant_dynamic-update-slice_fusion.1
  167.3 31.3 %collective-permute-done.2 = bf16[16,2,2,128,128]{4,3,2,1,0:T(8,128)(2,1)} collective-permute-done((bf16[16,2,2,128,128]{4,3,2,1,0:T(8,128)(2,1)}, bf16[16,2,2,128,128]{4,3,2,1,0:T(8,128)(2,1)}, u32[]{:S(2)}, u32[]{:S(2)}) %collective-permute-start.2) | collective-permute-done | bytes 2097184 | tf_op jit(solution)/shard_map/ppermute | solution.py:26
  198.6 3.2 constant_dynamic-update-slice_fusion
  201.8 18.4 %convolution_bitcast_fusion.2 = f32[16,2,4,2,2,128,128]{6,5,4,2,3,1,0:T(8,128)} fusion(bf16[1,64,4,2,128,128]{5,4,3,2,1,0:T(8,128)(2,1)} %bitcast.150, bf16[64,2,2,128,128]{4,3,2,1,0:T(8,128)(2,1)} %constant_dynamic-update-slice_fusion), kind=kOutput, calls=%fused_computation.10 | convolution fusion | flops 2147483648 | bytes 39845888 | tf_op jit(solution)/shard_map/kmcij,kndjl->kmncdil/dot_general | solution.py:50
  220.2 18.9 %convolution_bitcast_fusion.3 = f32[16,2,4,2,2,128,128]{6,5,4,2,3,1,0:T(8,128)} fusion(bf16[1,64,4,2,128,128]{5,4,3,2,1,0:T(8,128)(2,1)} %bitcast.151, bf16[64,2,2,128,128]{4,3,2,1,0:T(8,128)(2,1)} %constant_dynamic-update-slice_fusion), kind=kOutput, calls=%fused_computation.11 | convolution fusion | flops 2147483648 | bytes 39845888 | tf_op jit(solution)/shard_map/kmcij,kndjl->kmncdil/dot_general | solution.py:50
  239.1 18.4 %convolution_bitcast_fusion.1 = f32[16,2,4,2,2,128,128]{6,5,4,2,3,1,0:T(8,128)} fusion(bf16[1,64,4,2,128,128]{5,4,3,2,1,0:T(8,128)(2,1)} %bitcast.152, bf16[64,2,2,128,128]{4,3,2,1,0:T(8,128)(2,1)} %constant_dynamic-update-slice_fusion), kind=kOutput, calls=%fused_computation.9 | convolution fusion | flops 2147483648 | bytes 39845888 | tf_op jit(solution)/shard_map/kmcij,kndjl->kmncdil/dot_general | solution.py:50
  257.5 18.4 %convolution_bitcast_fusion = f32[16,2,4,2,2,128,128]{6,5,4,2,3,1,0:T(8,128)} fusion(bf16[1,64,4,2,128,128]{5,4,3,2,1,0:T(8,128)(2,1)} %bitcast.153, bf16[64,2,2,128,128]{4,3,2,1,0:T(8,128)(2,1)} %constant_dynamic-update-slice_fusion), kind=kOutput, calls=%fused_computation.8 | convolution fusion | flops 2147483648 | bytes 39845888 | tf_op jit(solution)/shard_map/kmcij,kndjl->kmncdil/dot_general | solution.py:50
  275.9 19.3 %slice_subtract_fusion.2 = (f32[16,2,4,1,1,128,128]{6,5,4,2,3,1,0:T(8,128)}, f32[16,2,4,1,1,128,128]{6,5,4,2,3,1,0:T(8,128)}) fusion(f32[16,2,4,2,2,128,128]{6,5,4,2,3,1,0:T(8,128)} %convolution_bitcast_fusion.2), kind=kLoop, calls=%fused_computation.17 | loop fusion | flops 4194304 | bytes 50331648 | tf_op jit(solution)/shard_map/sub | solution.py:53
  295.2 19.4 %slice_subtract_fusion.3 = (f32[16,2,4,1,1,128,128]{6,5,4,2,3,1,0:T(8,128)}, f32[16,2,4,1,1,128,128]{6,5,4,2,3,1,0:T(8,128)}) fusion(f32[16,2,4,2,2,128,128]{6,5,4,2,3,1,0:T(8,128)} %convolution_bitcast_fusion.3), kind=kLoop, calls=%fused_computation.19 | loop fusion | flops 4194304 | bytes 50331648 | tf_op jit(solution)/shard_map/sub | solution.py:53
  314.5 19.2 %slice_subtract_fusion.1 = (f32[16,2,4,1,1,128,128]{6,5,4,2,3,1,0:T(8,128)}, f32[16,2,4,1,1,128,128]{6,5,4,2,3,1,0:T(8,128)}) fusion(f32[16,2,4,2,2,128,128]{6,5,4,2,3,1,0:T(8,128)} %convolution_bitcast_fusion.1), kind=kLoop, calls=%fused_computation.15 | loop fusion | flops 4194304 | bytes 50331648 | tf_op jit(solution)/shard_map/sub | solution.py:53
  333.7 19.1 %slice_subtract_fusion = (f32[16,2,4,1,1,128,128]{6,5,4,2,3,1,0:T(8,128)}, f32[16,2,4,1,1,128,128]{6,5,4,2,3,1,0:T(8,128)}) fusion(f32[16,2,4,2,2,128,128]{6,5,4,2,3,1,0:T(8,128)} %convolution_bitcast_fusion), kind=kLoop, calls=%fused_computation.13 | loop fusion | flops 4194304 | bytes 50331648 | tf_op jit(solution)/shard_map/sub | solution.py:53
  352.9 13.8 %maximum_multiply_fusion.1 = f32[128,2,128,128]{3,2,1,0:T(8,128)} fusion(f32[128,1,128,128]{3,2,1,0:T(8,128)} %bitcast.149, f32[128,1,128,128]{3,2,1,0:T(8,128)} %bitcast.148, f32[128]{0:T(128)S(1)} %reshape.717), kind=kLoop, calls=%fused_computation.5 | loop fusion | flops 8388608 | bytes 33554944 | tf_op jit(solution)/shard_map/mul | solution.py:55
  366.7 2.6 copy-done.1
  369.4 6.3 %maximum_multiply_fusion = f32[128,2,128,128]{3,2,1,0:T(8,128)} fusion(f32[128,1,128,128]{3,2,1,0:T(8,128)S(1)} %bitcast.147, f32[128,1,128,128]{3,2,1,0:T(8,128)S(1)} %bitcast.146, f32[128]{0:T(128)S(1)} %reshape.716), kind=kLoop, calls=%fused_computation.4 | loop fusion | flops 8388608 | bytes 33554944 | tf_op jit(solution)/shard_map/mul | solution.py:55
  375.6 7.9 %broadcast_in_dim.28 = f32[8,16,2,128,128]{4,3,2,1,0:T(8,128)} broadcast(f32[]{:T(128)} %constant.36.clone.1), dimensions={} | broadcast | bytes 16777220 | tf_op jit(solution)/shard_map/broadcast_in_dim | solution.py:83
  383.5 39.5 %scatter_fusion = f32[8,16,2,128,128]{4,3,2,1,0:T(8,128)} fusion(f32[8,16,2,128,128]{4,3,2,1,0:T(8,128)} %broadcast_in_dim.28, s32[128]{0:T(128)S(1)} %get-tuple-element.37, f32[128,2,128,128]{3,2,1,0:T(8,128)} %maximum_multiply_fusion), kind=kCustom, calls=%fused_computation | custom fusion | flops 4194304 | bytes 50332672 | tf_op jit(solution)/shard_map/scatter-add | solution.py:61
  423.0 39.7 %scatter_fusion.1 = f32[8,16,2,128,128]{4,3,2,1,0:T(8,128)} fusion(f32[8,16,2,128,128]{4,3,2,1,0:T(8,128)} %scatter_fusion, s32[128]{0:T(128)S(1)} %copy-done.4, f32[128,2,128,128]{3,2,1,0:T(8,128)} %maximum_multiply_fusion.1), kind=kCustom, calls=%fused_computation.1 | custom fusion | flops 4194304 | bytes 50332672 | tf_op jit(solution)/shard_map/scatter-add | solution.py:61
  462.7 12.0 %maximum_multiply_fusion.2 = f32[128,2,128,128]{3,2,1,0:T(8,128)} fusion(f32[128,1,128,128]{3,2,1,0:T(8,128)} %bitcast.145, f32[128,1,128,128]{3,2,1,0:T(8,128)} %bitcast.144, f32[128]{0:T(128)S(1)} %copy-done.6), kind=kLoop, calls=%fused_computation.6 | loop fusion | flops 8388608 | bytes 33554944 | tf_op jit(solution)/shard_map/mul | solution.py:55
  474.7 39.6 %scatter_fusion.2 = f32[8,16,2,128,128]{4,3,2,1,0:T(8,128)} fusion(f32[8,16,2,128,128]{4,3,2,1,0:T(8,128)} %scatter_fusion.1, s32[128]{0:T(128)S(1)} %copy-done.3, f32[128,2,128,128]{3,2,1,0:T(8,128)} %maximum_multiply_fusion.2), kind=kCustom, calls=%fused_computation.2 | custom fusion | flops 4194304 | bytes 50332672 | tf_op jit(solution)/shard_map/scatter-add | solution.py:61
  514.3 12.0 %maximum_multiply_fusion.3 = f32[128,2,128,128]{3,2,1,0:T(8,128)} fusion(f32[128,1,128,128]{3,2,1,0:T(8,128)} %bitcast.143, f32[128,1,128,128]{3,2,1,0:T(8,128)} %bitcast.142, f32[128]{0:T(128)S(1)} %copy-done.7), kind=kLoop, calls=%fused_computation.7 | loop fusion | flops 8388608 | bytes 33554944 | tf_op jit(solution)/shard_map/mul | solution.py:55
  526.3 39.6 %scatter_fusion.3 = f32[8,16,2,128,128]{4,3,2,1,0:T(8,128)} fusion(f32[8,16,2,128,128]{4,3,2,1,0:T(8,128)} %scatter_fusion.2, s32[128]{0:T(128)S(1)} %copy-done.2, f32[128,2,128,128]{3,2,1,0:T(8,128)} %maximum_multiply_fusion.3), kind=kCustom, calls=%fused_computation.3 | custom fusion | flops 4194304 | bytes 50332672 | tf_op jit(solution)/shard_map/scatter-add | solution.py:61
  565.9 9.2 %convert_element_type.55 = bf16[8,16,2,128,128]{4,3,2,1,0:T(8,128)(2,1)} convert(f32[8,16,2,128,128]{4,3,2,1,0:T(8,128)} %scatter_fusion.3) | non-fusion elementwise | flops 4194304 | bytes 25165824 | tf_op jit(solution)/shard_map/convert_element_type | solution.py:108
  (36 shorter events, 0.6 us)
Async XLA Ops:
  6.5 153.0 %copy-start.5 = (bf16[1,16,2,2,128,128]{5,4,3,2,1,0:T(8,128)(2,1)S(1)}, bf16[1,16,2,2,128,128]{5,4,3,2,1,0:T(8,128)(2,1)}, u32[]{:S(2)}) copy-start(bf16[1,16,2,2,128,128]{5,4,3,2,1,0:T(8,128)(2,1)} %param.8) | copy-start | bytes 6291460
  6.5 195.2 %all-gather.9.cloned.1.call-start = ((), (), s32[]{:S(2)}) async-start(), calls=%async_computation | async-start | bytes 20971520 | tf_op jit(solution)/shard_map/all_gather | solution.py:85
  7.3 49.8 %collective-permute-start = (bf16[16,2,2,128,128]{4,3,2,1,0:T(8,128)(2,1)}, bf16[16,2,2,128,128]{4,3,2,1,0:T(8,128)(2,1)}, u32[]{:S(2)}, u32[]{:S(2)}) collective-permute-start(bf16[16,2,2,128,128]{4,3,2,1,0:T(8,128)(2,1)} %bitcast.155), channel_id=1, source_target_pairs={{0,1},{1,2},{2,3},{3,0},{4,5},{5,6},{6,7},{7,4},{8,9},{9,10},{10,1... | collective-permute-start | bytes 6291464 | tf_op jit(solution)/shard_map/ppermute | solution.py:26
  57.1 92.3 %collective-permute-start.1 = (bf16[16,2,2,128,128]{4,3,2,1,0:T(8,128)(2,1)}, bf16[16,2,2,128,128]{4,3,2,1,0:T(8,128)(2,1)}, u32[]{:S(2)}, u32[]{:S(2)}) collective-permute-start(bf16[16,2,2,128,128]{4,3,2,1,0:T(8,128)(2,1)} %collective-permute-done), channel_id=1, source_target_pairs={{0,1},{1,2},{2,3},{3,0},{4,5},{5,6},{6,7},{7,4},{8,9},{9,10},{10,1... | collective-permute-start | bytes 6291464 | tf_op jit(solution)/shard_map/ppermute | solution.py:26
  149.4 49.2 %collective-permute-start.2 = (bf16[16,2,2,128,128]{4,3,2,1,0:T(8,128)(2,1)}, bf16[16,2,2,128,128]{4,3,2,1,0:T(8,128)(2,1)}, u32[]{:S(2)}, u32[]{:S(2)}) collective-permute-start(bf16[16,2,2,128,128]{4,3,2,1,0:T(8,128)(2,1)} %collective-permute-done.1), channel_id=1, source_target_pairs={{0,1},{1,2},{2,3},{3,0},{4,5},{5,6},{6,7},{7,4},{8,9},{9,10},{10,1... | collective-permute-start | bytes 6291464 | tf_op jit(solution)/shard_map/ppermute | solution.py:26
  352.9 13.8 %copy-start = (f32[16,2,4,1,1,128,128]{6,5,4,2,3,1,0:T(8,128)S(1)}, f32[16,2,4,1,1,128,128]{6,5,4,2,3,1,0:T(8,128)}, u32[]{:S(2)}) copy-start(f32[16,2,4,1,1,128,128]{6,5,4,2,3,1,0:T(8,128)} %get-tuple-element.11) | copy-start | bytes 25165828
  352.9 16.5 %copy-start.1 = (f32[16,2,4,1,1,128,128]{6,5,4,2,3,1,0:T(8,128)S(1)}, f32[16,2,4,1,1,128,128]{6,5,4,2,3,1,0:T(8,128)}, u32[]{:S(2)}) copy-start(f32[16,2,4,1,1,128,128]{6,5,4,2,3,1,0:T(8,128)} %get-tuple-element.12) | copy-start | bytes 25165828
  383.5 39.5 %copy-start.4 = (s32[128]{0:T(128)S(1)}, s32[128]{0:T(128)}, u32[]{:S(2)}) copy-start(s32[128]{0:T(128)} %get-tuple-element.38) | copy-start | bytes 1540
  423.0 39.7 %copy-start.6 = (f32[128]{0:T(128)S(1)}, f32[128]{0:T(128)}, u32[]{:S(2)}) copy-start(f32[128]{0:T(128)} %reshape.718) | copy-start | bytes 1540
  462.7 12.0 %copy-start.3 = (s32[128]{0:T(128)S(1)}, s32[128]{0:T(128)}, u32[]{:S(2)}) copy-start(s32[128]{0:T(128)} %get-tuple-element.39) | copy-start | bytes 1540
  474.7 39.6 %copy-start.7 = (f32[128]{0:T(128)S(1)}, f32[128]{0:T(128)}, u32[]{:S(2)}) copy-start(f32[128]{0:T(128)} %reshape.719) | copy-start | bytes 1540
  514.3 12.0 %copy-start.2 = (s32[128]{0:T(128)S(1)}, s32[128]{0:T(128)}, u32[]{:S(2)}) copy-start(s32[128]{0:T(128)} %get-tuple-element.40) | copy-start | bytes 1540
Sparse Core Ops, SparseCore 0:
  8.9 108.3 all-gather.8
